TPU v7x, 256 devices: a whole 4x4x8 slice. The times are simulated.
256 devices in a mesh: pair: 32 (over x, z_hi, core), aux: 8 (over z_lo, y).
Axes of the slice: x: 4, y: 4, z: 8 (z_hi: 4, z_lo: 2; z = z_hi * 2 + z_lo), core: 2. Of those that a mesh axis runs over, the one named last changes fastest.
Arguments:
- integrals: float32 [32, 640, 4096], P(None, 'aux', 'pair'), may hold values from -6 to 6
- factor: float32 [4096, 4096], P('aux', 'pair'), may hold values from -1 to 2, as said below
- diag_inverse: float32 [8, 512, 512], P('aux'), may hold values from -1 to 1, as said below
Outputs:
- transformed: float32 [32, 640, 4096], P('pair', None, 'aux')
Inputs may be any that keep to these rules, and one draw needn't show every extreme that they name: factor is zero above its diagonal. diag_inverse[j] is the inverse, up to rounding, of the factor's j-th diagonal block of 512 x 512.
All inputs are finite; a program needn't handle non-finite values.
Results may differ from a plain program's by a relative error of at most 0.0001.
Values sent between devices are 32-bit elements; how exact they have to be, the bound alone decides.
No kernel may reach another device: no remote copies, remote signals or barrier semaphores. Data moves between devices by JAX's collectives and lax.ppermute only.
A program may use at most 128 MiB of HBM per device.

v0:
```python
import jax
import jax.numpy as jnp
from jax import lax
from jax.sharding import PartitionSpec as P


def from_root(x, axis, root):
    mine = lax.axis_index(axis) == root
    return lax.psum(jnp.where(mine, x, jnp.zeros_like(x)), axis)


def product(left, right):
    return jnp.dot(left, right, precision=lax.Precision.HIGHEST, preferred_element_type=jnp.float32)


def local(integrals, factor, diag_inverse):
    relaid = lax.all_to_all(
        lax.all_to_all(integrals, "pair", split_axis=0, concat_axis=2, tiled=True),
        "aux",
        split_axis=2,
        concat_axis=1,
        tiled=True,
    )
    occ_count, virt_count, panel_width = relaid.shape
    remain = relaid.reshape(occ_count * virt_count, panel_width)
    row_panel = lax.all_gather(factor, "pair", axis=1, tiled=True)
    inverse_t = diag_inverse[0].T
    own_index = lax.axis_index("aux")
    panel_count = lax.axis_size("aux")
    result = jnp.zeros_like(remain)
    for step in range(panel_count):
        result = lax.cond(own_index == step, lambda: product(remain, inverse_t), lambda: result)
        if step + 1 < panel_count:
            factor_block = row_panel[:, step * panel_width : (step + 1) * panel_width].T
            arrived = from_root(result, "aux", step)
            remain = lax.cond(
                own_index > step, lambda: remain - product(arrived, factor_block), lambda: remain
            )
    return result.reshape(occ_count, virt_count, panel_width)


def solution(mesh):
    in_specs = (P(None, "aux", "pair"), P("aux", "pair"), P("aux", None, None))
    out_specs = P("pair", None, "aux")
    return jax.shard_map(local, mesh=mesh, in_specs=in_specs, out_specs=out_specs, check_vma=False)
```

profile of v0, /device:TPU:56, one launch (start us, length us, event | category | flops | bytes accessed | tf_op | source)
XLA Modules:
  0.0 783.9 jit_solution(10869943194843136534)
XLA Ops:
  7.4 1.8 copy.26
  9.2 53.9 %all_to_all.33 = f32[32,80,128]{2,1,0:T(8,128)S(1)} all-to-all(f32[32,80,128]{2,1,0:T(8,128)} %param.33), channel_id=1, replica_groups=mesh['pair'=32,'aux'=8] {'pair'}, dimensions={0} | all-to-all | bytes 2621440 | tf_op jit(solution)/shard_map/all_to_all | solution.py:18
  63.5 5.1 copy.22
  68.7 5.7 all-to-all-start.1
  74.7 52.9 %all-to-all-done.1 = f32[1,80,4096]{1,0,2:T(1,128)} async-done(((f32[1,80,4096]{1,0,2:T(1,128)}), f32[1,80,4096]{1,0,2:T(1,128)}, u32[]{:S(2)}, u32[]{:S(2)}) %all-to-all-start.1) | async-done | bytes 1310752 | tf_op jit(solution)/shard_map/all_to_all | solution.py:17
  127.6 2.8 copy.27
  130.4 2.1 copy.24
  132.5 1.2 conditional.15
  135.0 6.2 slice_bitcast_fusion
  141.2 77.3 %all-reduce.8.cloned.1.call-done = f32[640,512]{1,0:T(8,128)} async-done(((f32[640,512]{1,0:T(8,128)}), f32[640,512]{1,0:T(8,128)}) %all-reduce.8.cloned.1.call-update) | async-done | bytes 1310736 | tf_op jit(solution)/shard_map/psum | solution.py:9
  218.5 4.0 conditional.16
  218.5 4.0 convolution_subtract_fusion
  223.8 85.2 %all-reduce.10.cloned.1.call-done = f32[640,512]{1,0:T(8,128)} async-done(((f32[640,512]{1,0:T(8,128)}), f32[640,512]{1,0:T(8,128)}) %all-reduce.10.cloned.1.call-update) | async-done | bytes 1310736 | tf_op jit(solution)/shard_map/psum | solution.py:9
  309.0 4.5 conditional.18
  309.5 4.0 convolution_subtract_fusion.1
  314.8 87.7 %all-reduce.12.cloned.1.call-done = f32[640,512]{1,0:T(8,128)} async-done(((f32[640,512]{1,0:T(8,128)}), f32[640,512]{1,0:T(8,128)}) %all-reduce.12.cloned.1.call-update) | async-done | bytes 1310736 | tf_op jit(solution)/shard_map/psum | solution.py:9
  402.5 4.0 conditional.20
  402.5 4.0 convolution_subtract_fusion.2
  407.8 87.0 %all-reduce.14.cloned.1.call-done = f32[640,512]{1,0:T(8,128)} async-done(((f32[640,512]{1,0:T(8,128)}), f32[640,512]{1,0:T(8,128)}) %all-reduce.14.cloned.1.call-update) | async-done | bytes 1310736 | tf_op jit(solution)/shard_map/psum | solution.py:9
  494.8 4.0 conditional.22
  494.8 4.0 convolution_subtract_fusion.3
  500.3 86.1 %all-reduce.16.cloned.1.call-done = f32[640,512]{1,0:T(8,128)} async-done(((f32[640,512]{1,0:T(8,128)}), f32[640,512]{1,0:T(8,128)}) %all-reduce.16.cloned.1.call-update) | async-done | bytes 1310736 | tf_op jit(solution)/shard_map/psum | solution.py:9
  586.4 4.0 conditional.24
  586.4 4.0 convolution_subtract_fusion.4
  591.7 85.0 %all-reduce.18.cloned.1.call-done = f32[640,512]{1,0:T(8,128)} async-done(((f32[640,512]{1,0:T(8,128)}), f32[640,512]{1,0:T(8,128)}) %all-reduce.18.cloned.1.call-update) | async-done | bytes 1310736 | tf_op jit(solution)/shard_map/psum | solution.py:9
  676.7 4.0 conditional.26
  676.7 4.0 convolution_subtract_fusion.5
  682.0 87.0 %all-reduce.20.cloned.1.call-done = f32[640,512]{1,0:T(8,128)} async-done(((f32[640,512]{1,0:T(8,128)}), f32[640,512]{1,0:T(8,128)}) %all-reduce.20.cloned.1.call-update) | async-done | bytes 1310736 | tf_op jit(solution)/shard_map/psum | solution.py:9
  768.9 3.9 conditional.28
  769.1 3.7 convolution_subtract_fusion.6
  772.9 3.3 conditional.29
  772.9 3.3 convolution_bitcast_fusion
  (35 shorter events, 11.0 us)
Async XLA Ops:
  7.4 127.7 %all-gather.2.cloned.1.call-start = ((), (), s32[]{:S(2)}) async-start(), calls=%async_computation.3 | async-start | bytes 8650752 | tf_op jit(solution)/shard_map/all_gather | solution.py:26
  68.7 5.7 copy-start
  68.7 59.0 %all-to-all-start.1 = ((f32[1,80,4096]{1,0,2:T(1,128)}), f32[1,80,4096]{1,0,2:T(1,128)}, u32[]{:S(2)}, u32[]{:S(2)}) async-start(f32[1,80,4096]{1,0,2:T(1,128)} %copy.22), calls=%async_computation.1 | async-start | bytes 4194304 | tf_op jit(solution)/shard_map/all_to_all | solution.py:17
  74.4 144.1 %all-reduce.8.cloned.1.call-start = ((), (), s32[]{:S(2)}) async-start(), calls=%async_computation.2 | async-start | bytes 2621440 | tf_op jit(solution)/shard_map/psum | solution.py:9
  135.0 174.1 %all-reduce.10.cloned.1.call-start = ((), (), s32[]{:S(2)}) async-start(), calls=%async_computation.4 | async-start | bytes 2621440 | tf_op jit(solution)/shard_map/psum | solution.py:9
  223.7 178.7 %all-reduce.12.cloned.1.call-start = ((), (), s32[]{:S(2)}) async-start(), calls=%async_computation.5 | async-start | bytes 2621440 | tf_op jit(solution)/shard_map/psum | solution.py:9
  314.7 180.1 %all-reduce.14.cloned.1.call-start = ((), (), s32[]{:S(2)}) async-start(), calls=%async_computation.6 | async-start | bytes 2621440 | tf_op jit(solution)/shard_map/psum | solution.py:9
  407.8 178.6 %all-reduce.16.cloned.1.call-start = ((), (), s32[]{:S(2)}) async-start(), calls=%async_computation.7 | async-start | bytes 2621440 | tf_op jit(solution)/shard_map/psum | solution.py:9
  500.3 176.4 %all-reduce.18.cloned.1.call-start = ((), (), s32[]{:S(2)}) async-start(), calls=%async_computation.8 | async-start | bytes 2621440 | tf_op jit(solution)/shard_map/psum | solution.py:9
  591.7 177.3 %all-reduce.20.cloned.1.call-start = ((), (), s32[]{:S(2)}) async-start(), calls=%async_computation.9 | async-start | bytes 2621440 | tf_op jit(solution)/shard_map/psum | solution.py:9
Sparse Core Ops, SparseCore 0:
  10.7 112.6 all-gather.1
Sparse Core Ops, SparseCore 1:
  135.0 83.4 all-reduce.7
  223.8 85.1 all-reduce.9
  314.8 87.6 all-reduce.11
  407.8 86.9 all-reduce.13
  500.4 86.0 all-reduce.15
  591.8 84.9 all-reduce.17
  682.1 86.8 all-reduce.19
where the time goes:
time: 792 us; the launch traced here: 784 us
  waiting for transfers between devices  648 us (82%)
  blocking collectives  53.9 us (7%)
  matrix products  31.2 us (4%)
  local copies, waits for them, and re-layouts  19.9 us (3%)
  between operations  15.3 us (2%)
  other arithmetic  8.41 us (1%)
    psum x7, waiting for transfers between devices, from_root(): return lax.psum(jnp.where(mine, x, jnp.zeros_like(x)), axis)  595 us
    all_to_all x1, blocking collectives, local(): lax.all_to_all(integrals, 'pair', split_axis=0, concat_axis=2, tiled=True)  53.9 us
    all_to_all x1, waiting for transfers between devices, local(): lax.all_to_all(lax.all_to_all(integrals, 'pair', split_axis=0, concat_axi...  52.9 us
    dot_general x8, matrix products, product(): jnp.dot(left, right, precision=lax.Precision.HIGHEST, preferred_element_t...  31.2 us
  transfers between devices with their start and end apart: 9, of which 8 were waited for; matrix products, arithmetic and copies ran while one was open for 2% of the time, Pallas kernels for 0%

commit v1 on v0

--- a/solution.py
+++ b/solution.py
@@ -14,12 +14,20 @@
 
 
 def local(integrals, factor, diag_inverse):
-    relaid = lax.all_to_all(
-        lax.all_to_all(integrals, "pair", split_axis=0, concat_axis=2, tiled=True),
-        "aux",
-        split_axis=2,
-        concat_axis=1,
-        tiled=True,
+    relaid = jnp.concatenate(
+        lax.all_to_all(
+            jnp.stack(
+                jnp.split(
+                    lax.all_to_all(integrals, "pair", split_axis=0, concat_axis=2, tiled=True),
+                    lax.axis_size("aux"),
+                    axis=2,
+                )
+            ),
+            "aux",
+            0,
+            0,
+        ),
+        axis=1,
     )
     occ_count, virt_count, panel_width = relaid.shape
     remain = relaid.reshape(occ_count * virt_count, panel_width)

time: 792 us -> 776 us (0.980)
  waiting for transfers between devices: 648 us -> 637 us
    all_to_all x1, waiting for transfers between devices: 52.9 us -> 44.6 us  [local(): lax.all_to_all(jnp.stack(jnp.split(lax.all_to_all(integrals, 'pair', spli...]
  transfers between devices with their start and end apart: 9 -> 9, of which waited for: 8 -> 9; matrix products, arithmetic and copies ran while one was open for 2% -> 2% of each run, Pallas kernels for 0% -> 0%
where the time goes in v1:
time: 776 us; the launch traced here: 768 us
  waiting for transfers between devices  637 us (82%)
  blocking collectives  54.1 us (7%)
  matrix products  31.2 us (4%)
  between operations  15.3 us (2%)
  local copies, waits for them, and re-layouts  14.8 us (2%)
  other arithmetic  8.49 us (1%)
    psum x7, waiting for transfers between devices, from_root(): return lax.psum(jnp.where(mine, x, jnp.zeros_like(x)), axis)  591 us
    all_to_all x1, blocking collectives, local(): lax.all_to_all(integrals, 'pair', split_axis=0, concat_axis=2, tiled=True)  54.1 us
    all_to_all x1, waiting for transfers between devices, local(): lax.all_to_all(jnp.stack(jnp.split(lax.all_to_all(integrals, 'pair', spli...  44.6 us
    dot_general x8, matrix products, product(): jnp.dot(left, right, precision=lax.Precision.HIGHEST, preferred_element_t...  31.2 us
  transfers between devices with their start and end apart: 9, of which 9 were waited for; matrix products, arithmetic and copies ran while one was open for 2% of the time, Pallas kernels for 0%

profile of v1, /device:TPU:56, one launch (start us, length us, event | category | flops | bytes accessed | tf_op | source)
XLA Modules:
  0.0 767.7 jit_solution(4415548865159199285)
XLA Ops:
  7.4 1.8 copy.25
  9.2 54.1 %all_to_all.23 = f32[32,80,128]{2,1,0:T(8,128)S(1)} all-to-all(f32[32,80,128]{2,1,0:T(8,128)} %param.33), channel_id=1, replica_groups=mesh['pair'=32,'aux'=8] {'pair'}, dimensions={0} | all-to-all | bytes 2621440 | tf_op jit(solution)/shard_map/all_to_all | solution.py:21
  64.8 2.0 stack.35
  66.8 1.8 copy.23
  68.6 5.5 all-to-all-start.1
  74.5 44.6 %all-to-all-done.1 = f32[8,1,80,512]{3,2,1,0:T(8,128)S(1)} async-done(((f32[8,1,80,512]{3,2,1,0:T(8,128)}), f32[8,1,80,512]{3,2,1,0:T(8,128)S(1)}, u32[]{:S(2)}, u32[]{:S(2)}) %all-to-all-start.1) | async-done | bytes 1310752 | tf_op jit(solution)/shard_map/all_to_all | solution.py:18
  119.1 1.2 conditional.15
  121.6 1.3 all-gather.2.cloned.1.call-done
  122.9 6.2 slice_bitcast_fusion
  129.1 73.1 %all-reduce.8.cloned.1.call-done = f32[640,512]{1,0:T(8,128)} async-done(((f32[640,512]{1,0:T(8,128)}), f32[640,512]{1,0:T(8,128)}) %all-reduce.8.cloned.1.call-update) | async-done | bytes 1310736 | tf_op jit(solution)/shard_map/psum | solution.py:9
  202.2 4.0 conditional.16
  202.2 4.0 convolution_subtract_fusion
  207.6 85.2 %all-reduce.10.cloned.1.call-done = f32[640,512]{1,0:T(8,128)} async-done(((f32[640,512]{1,0:T(8,128)}), f32[640,512]{1,0:T(8,128)}) %all-reduce.10.cloned.1.call-update) | async-done | bytes 1310736 | tf_op jit(solution)/shard_map/psum | solution.py:9
  292.8 4.5 conditional.18
  293.2 4.0 convolution_subtract_fusion.1
  298.6 87.7 %all-reduce.12.cloned.1.call-done = f32[640,512]{1,0:T(8,128)} async-done(((f32[640,512]{1,0:T(8,128)}), f32[640,512]{1,0:T(8,128)}) %all-reduce.12.cloned.1.call-update) | async-done | bytes 1310736 | tf_op jit(solution)/shard_map/psum | solution.py:9
  386.3 4.0 conditional.20
  386.3 4.0 convolution_subtract_fusion.2
  391.6 87.0 %all-reduce.14.cloned.1.call-done = f32[640,512]{1,0:T(8,128)} async-done(((f32[640,512]{1,0:T(8,128)}), f32[640,512]{1,0:T(8,128)}) %all-reduce.14.cloned.1.call-update) | async-done | bytes 1310736 | tf_op jit(solution)/shard_map/psum | solution.py:9
  478.6 4.0 conditional.22
  478.6 4.0 convolution_subtract_fusion.3
  484.1 86.0 %all-reduce.16.cloned.1.call-done = f32[640,512]{1,0:T(8,128)} async-done(((f32[640,512]{1,0:T(8,128)}), f32[640,512]{1,0:T(8,128)}) %all-reduce.16.cloned.1.call-update) | async-done | bytes 1310736 | tf_op jit(solution)/shard_map/psum | solution.py:9
  570.2 4.0 conditional.24
  570.2 4.0 convolution_subtract_fusion.4
  575.5 85.0 %all-reduce.18.cloned.1.call-done = f32[640,512]{1,0:T(8,128)} async-done(((f32[640,512]{1,0:T(8,128)}), f32[640,512]{1,0:T(8,128)}) %all-reduce.18.cloned.1.call-update) | async-done | bytes 1310736 | tf_op jit(solution)/shard_map/psum | solution.py:9
  660.5 4.0 conditional.26
  660.5 4.0 convolution_subtract_fusion.5
  665.8 86.9 %all-reduce.20.cloned.1.call-done = f32[640,512]{1,0:T(8,128)} async-done(((f32[640,512]{1,0:T(8,128)}), f32[640,512]{1,0:T(8,128)}) %all-reduce.20.cloned.1.call-update) | async-done | bytes 1310736 | tf_op jit(solution)/shard_map/psum | solution.py:9
  752.7 3.9 conditional.28
  752.9 3.7 convolution_subtract_fusion.6
  756.7 3.3 conditional.29
  756.7 3.3 convolution_bitcast_fusion
  (35 shorter events, 12.1 us)
Async XLA Ops:
  7.4 115.5 %all-gather.2.cloned.1.call-start = ((), (), s32[]{:S(2)}) async-start(), calls=%async_computation.3 | async-start | bytes 8650752 | tf_op jit(solution)/shard_map/all_gather | solution.py:34
  68.6 5.5 copy-start
  68.6 50.5 %all-to-all-start.1 = ((f32[8,1,80,512]{3,2,1,0:T(8,128)}), f32[8,1,80,512]{3,2,1,0:T(8,128)S(1)}, u32[]{:S(2)}, u32[]{:S(2)}) async-start(f32[8,1,80,512]{3,2,1,0:T(8,128)} %copy.23), calls=%async_computation.1 | async-start | bytes 2621440 | tf_op jit(solution)/shard_map/all_to_all | solution.py:18
  74.2 128.1 %all-reduce.8.cloned.1.call-start = ((), (), s32[]{:S(2)}) async-start(), calls=%async_computation.2 | async-start | bytes 2621440 | tf_op jit(solution)/shard_map/psum | solution.py:9
  121.5 171.3 %all-reduce.10.cloned.1.call-start = ((), (), s32[]{:S(2)}) async-start(), calls=%async_computation.4 | async-start | bytes 2621440 | tf_op jit(solution)/shard_map/psum | solution.py:9
  207.5 178.7 %all-reduce.12.cloned.1.call-start = ((), (), s32[]{:S(2)}) async-start(), calls=%async_computation.5 | async-start | bytes 2621440 | tf_op jit(solution)/shard_map/psum | solution.py:9
  298.5 180.1 %all-reduce.14.cloned.1.call-start = ((), (), s32[]{:S(2)}) async-start(), calls=%async_computation.6 | async-start | bytes 2621440 | tf_op jit(solution)/shard_map/psum | solution.py:9
  391.5 178.6 %all-reduce.16.cloned.1.call-start = ((), (), s32[]{:S(2)}) async-start(), calls=%async_computation.7 | async-start | bytes 2621440 | tf_op jit(solution)/shard_map/psum | solution.py:9
  484.1 176.4 %all-reduce.18.cloned.1.call-start = ((), (), s32[]{:S(2)}) async-start(), calls=%async_computation.8 | async-start | bytes 2621440 | tf_op jit(solution)/shard_map/psum | solution.py:9
  575.5 177.3 %all-reduce.20.cloned.1.call-start = ((), (), s32[]{:S(2)}) async-start(), calls=%async_computation.9 | async-start | bytes 2621440 | tf_op jit(solution)/shard_map/psum | solution.py:9
Sparse Core Ops, SparseCore 0:
  10.7 112.1 all-gather.1
Sparse Core Ops, SparseCore 1:
  121.6 80.6 all-reduce.7
  207.6 85.1 all-reduce.9
  298.6 87.6 all-reduce.11
  391.6 86.9 all-reduce.13
  484.2 86.0 all-reduce.15
  575.6 84.9 all-reduce.17
  665.9 86.8 all-reduce.19
